TPU v7x, 32 devices: a whole 2x2x4 slice. The times are simulated.
32 devices in a mesh: row: 8 (over y, x, core), col: 4 (over z).
Axes of the slice: x: 2, y: 2, z: 4, core: 2. Of those that a mesh axis runs over, the one named last changes fastest.
Arguments:
- signal: float32 [128, 128, 16, 256], P('row', 'col'), may hold values from -40 to 40, as said below
- start_frames: float32 [256, 32], replicated, may hold values from -6 to 6
- start_sends: float32 [16, 8], replicated, may hold values from -6 to 6
- start_rows: float32 [128, 64], replicated, may hold values from -6 to 6
- start_cols: float32 [128, 64], replicated, may hold values from -6 to 6
- rank_frames: int32 [1], replicated, may hold values from 16 to 32
- rank_sends: int32 [1], replicated, may hold values from 4 to 8
Outputs:
- filtered: float32 [128, 128, 16, 256], P('row', 'col')
Inputs may be any that keep to these rules, and one draw needn't show every extreme that they name: `signal`: beamformed samples.
All inputs are finite; a program needn't handle non-finite values.
Results may differ from a plain program's by a relative error of at most 0.0003.
Values sent between devices are 32-bit elements; how exact they have to be, the bound alone decides.
No kernel may reach another device: no remote copies, remote signals or barrier semaphores. Data moves between devices by JAX's collectives and lax.ppermute only.
A program may use at most 128 MiB of HBM per device.

v0:
```python
import jax
import jax.numpy as jnp
from jax import lax
from jax.sharding import PartitionSpec as P

NT = 256
NK = 16
TMAX = 32
KMAX = 8
RS = 64
ITERS = 2
CORE_W = 256


def orthonormal(gram, start):
    high = lax.Precision.HIGHEST
    basis = start
    for rounds in range(ITERS):
        image = jnp.dot(gram, basis, precision=high)
        inner = jnp.dot(image.T, image, precision=high)
        factor = jnp.linalg.cholesky(inner)
        basis = jax.scipy.linalg.solve_triangular(factor, image.T, lower=True).T
    return basis


def local(signal, start_frames, start_sends, start_rows, start_cols, rank_frames, rank_sends):
    high = lax.Precision.HIGHEST
    rows_dev, cols_dev = (signal.shape[0], signal.shape[1])
    pixels = rows_dev * cols_dev
    flattened = signal.reshape(-1, NT)
    blocks = signal.reshape(pixels, NK, NT)
    local_frames = jnp.einsum("pt,pu->tu", flattened, flattened, precision=high)
    local_sends = jnp.einsum("pkt,pjt->kj", blocks, blocks, precision=high)
    gram_frames, gram_sends = lax.psum((local_frames, local_sends), ("row", "col"))
    keep_frames = (jnp.arange(TMAX, dtype=jnp.int32) < rank_frames[0]).astype(jnp.float32)
    keep_sends = (jnp.arange(KMAX, dtype=jnp.int32) < rank_sends[0]).astype(jnp.float32)
    basis_frames = orthonormal(gram_frames, start_frames) * keep_frames[None, :]
    basis_sends = orthonormal(gram_sends, start_sends) * keep_sends[None, :]
    reduced = jnp.dot(flattened, basis_frames, precision=high).reshape(pixels, NK, TMAX)
    core = jnp.einsum("pkb,ka->pab", reduced, basis_sends, precision=high)
    core = core.reshape(rows_dev, cols_dev, CORE_W)
    gathered = lax.all_gather(core, "row", axis=0, tiled=True)
    total_rows = gathered.shape[0]
    unfolded = gathered.reshape(total_rows, -1)
    local_rows = jnp.dot(unfolded, unfolded.T, precision=high)
    gram_rows = lax.psum(local_rows, "col")
    basis_rows = orthonormal(gram_rows, start_rows)
    second = jnp.dot(basis_rows.T, unfolded, precision=high).reshape(RS, cols_dev, CORE_W)
    width = CORE_W // lax.axis_size("row")
    own_slice = lax.dynamic_slice_in_dim(second, lax.axis_index("row") * width, width, 2)
    across = lax.all_gather(own_slice, "col", axis=1, tiled=True)
    local_cols = jnp.einsum("sce,sde->cd", across, across, precision=high)
    gram_cols = lax.psum(local_cols, "row")
    basis_cols = orthonormal(gram_cols, start_cols)
    third_slice = jnp.einsum("cu,sce->sue", basis_cols, across, precision=high)
    third = lax.all_gather(third_slice, "row", axis=2, tiled=True)
    cols_own = lax.dynamic_slice_in_dim(basis_cols, lax.axis_index("col") * cols_dev, cols_dev, 0)
    rows_own = lax.dynamic_slice_in_dim(basis_rows, lax.axis_index("row") * rows_dev, rows_dev, 0)
    back_cols = jnp.einsum("cu,sue->sce", cols_own, third, precision=high)
    tissue_core = jnp.dot(rows_own, back_cols.reshape(RS, -1), precision=high)
    tissue_core = tissue_core.reshape(pixels, KMAX, TMAX)
    expanded = jnp.einsum("pab,ka->pkb", tissue_core, basis_sends, precision=high)
    tissue = jnp.dot(expanded.reshape(-1, TMAX), basis_frames.T, precision=high).reshape(
        signal.shape
    )
    return signal - tissue


def solution(mesh):
    return jax.shard_map(
        local,
        mesh=mesh,
        in_specs=(P("row", "col", None, None), P(), P(), P(), P(), P(), P()),
        out_specs=P("row", "col", None, None),
        check_vma=False,
    )
```

profile of v0, /device:TPU:0, one launch (start us, length us, event | category | flops | bytes accessed | tf_op | source)
XLA Modules:
  0.0 528.9 jit_solution(3371056779634263745)
XLA Ops:
  6.5 17.7 %convolution_bitcast_fusion.4 = f32[256,256]{1,0:T(8,128)} fusion(f32[16,32,16,256]{3,2,1,0:T(8,128)} %param.16), kind=kOutput, calls=%fused_computation.9 | convolution fusion | flops 6442450944 | bytes 8650752 | tf_op jit(solution)/shard_map/pt,pu->tu/dot_general | solution.py:32
  24.3 14.1 %convolution_bitcast_fusion.6 = f32[16,16]{1,0:T(8,128)S(1)} fusion(f32[16,32,16,256]{3,2,1,0:T(8,128)} %param.16), kind=kOutput, calls=%fused_computation.13 | convolution fusion | flops 402653184 | bytes 8389632 | tf_op jit(solution)/shard_map/pkt,pjt->kj/dot_general | solution.py:33
  39.8 42.4 %psum.28 = f32[16,16]{1,0:T(8,128)S(1)} all-reduce(f32[16,16]{1,0:T(8,128)S(1)} %convolution_bitcast_fusion.6), channel_id=1, replica_groups=mesh['row'=8,'col'=4] {'row','col'}, use_global_device_ids=true, to_apply=%region_0.0 | all-reduce | flops 256 | bytes 2048 | tf_op jit(solution)/shard_map/psum | solution.py:34
  88.6 65.3 %all-reduce.4.cloned.1.call-done = f32[256,256]{1,0:T(8,128)} async-done(((f32[256,256]{1,0:T(8,128)}), f32[256,256]{1,0:T(8,128)}) %all-reduce.4.cloned.1.call-update) | async-done | bytes 262160 | tf_op jit(solution)/shard_map/psum | solution.py:34
  153.9 1.3 fusion.66
  155.5 2.9 cholesky.180
  159.7 2.4 custom-call.22
  162.4 1.3 fusion.68
  164.0 2.9 cholesky.191
  168.2 2.4 custom-call.23
  170.9 9.9 %convolution_bitcast_fusion = f32[8192,32]{0,1:T(8,128)S(1)} fusion(f32[32,256]{1,0:T(8,128)S(1)} %convolution_multiply_fusion, f32[8192,256]{1,0:T(8,128)} %bitcast.199), kind=kOutput, calls=%fused_computation | convolution fusion | flops 805306368 | bytes 9469952 | tf_op jit(solution)/shard_map/dot_general | solution.py:39
  180.8 2.7 copy.54
  183.5 3.2 copy.55
  187.4 0.8 copy.56
  188.8 1.1 copy.57
  190.2 35.5 %all-gather.4.cloned.1.call-done = f32[128,32,256]{2,0,1:T(8,128)} async-done(((f32[16,32,256]{2,0,1:T(8,128)}), f32[128,32,256]{2,0,1:T(8,128)}) %all-gather.4.cloned.1.call-update) | async-done | bytes 4194320 | tf_op jit(solution)/shard_map/all_gather | solution.py:42
  225.7 7.6 %convolution_bitcast_fusion.5 = f32[128,128]{1,0:T(8,128)} fusion(f32[128,32,256]{2,0,1:T(8,128)} %all-gather.4.cloned.1.call-done), kind=kOutput, calls=%fused_computation.11 | convolution fusion | flops 1610612736 | bytes 4259840 | tf_op jit(solution)/shard_map/dot_general | solution.py:45
  233.4 5.6 %copy.60 = f32[128,32,256]{0,2,1:T(8,128)} copy(f32[128,32,256]{2,0,1:T(8,128)} %all-gather.4.cloned.1.call-done) | data formatting | bytes 8388608 | tf_op jit(solution)/shard_map/all_gather | solution.py:42
  239.0 28.8 %all-reduce.6.cloned.1.call-done = f32[128,128]{1,0:T(8,128)} async-done(((f32[128,128]{1,0:T(8,128)}), f32[128,128]{1,0:T(8,128)}) %all-reduce.6.cloned.1.call-update) | async-done | bytes 65552 | tf_op jit(solution)/shard_map/psum | solution.py:46
  267.8 1.1 fusion.70
  269.2 5.8 %cholesky.202 = f32[64,64]{1,0:T(8,128)S(1)} custom-call(f32[64,64]{1,0:T(8,128)S(1)} %fusion.32), custom_call_target="Cholesky" | custom-call | tf_op jit(solution)/shard_map/jit(cholesky)/cholesky | solution.py:21
  275.1 0.7 compare_reduce_fusion.3
  276.5 4.9 custom-call.24
  281.6 1.1 fusion.72
  283.0 5.8 %cholesky.213 = f32[64,64]{1,0:T(8,128)S(1)} custom-call(f32[64,64]{1,0:T(8,128)S(1)} %fusion.28), custom_call_target="Cholesky" | custom-call | tf_op jit(solution)/shard_map/jit(cholesky)/cholesky | solution.py:21
  288.9 0.7 compare_reduce_fusion.2
  290.3 4.9 custom-call.25
  295.5 5.4 %fusion = f32[64,32,256]{0,2,1:T(8,128)S(1)} fusion(f32[128,32,256]{0,2,1:T(8,128)} %copy.60, f32[64,128]{1,0:T(8,128)S(1)} %fusion.25), kind=kOutput, calls=%fused_computation.1 | convolution fusion | flops 805306368 | bytes 6324224 | tf_op jit(solution)/shard_map/dot_general | solution.py:48
  300.9 0.8 constant_dynamic-slice_fusion
  302.2 45.0 %all-gather.6.cloned.1.call-done = f32[64,128,32]{0,2,1:T(8,128)} async-done(((f32[64,32,32]{0,2,1:T(8,128)}), f32[64,128,32]{0,2,1:T(8,128)}) %all-gather.6.cloned.1.call-update) | async-done | bytes 1048592 | tf_op jit(solution)/shard_map/all_gather | solution.py:51
  347.2 7.0 %fusion.4 = f32[128,128]{1,0:T(8,128)} fusion(f32[64,128,32]{0,2,1:T(8,128)} %all-gather.6.cloned.1.call-done), kind=kOutput, calls=%fused_computation.10 | convolution fusion | flops 402653184 | bytes 1114112 | tf_op jit(solution)/shard_map/sce,sde->cd/dot_general | solution.py:52
  354.3 3.0 copy.65
  357.4 49.1 %all-reduce.8.cloned.1.call-done = f32[128,128]{1,0:T(8,128)} async-done(((f32[128,128]{1,0:T(8,128)}), f32[128,128]{1,0:T(8,128)}) %all-reduce.8.cloned.1.call-update) | async-done | bytes 65552 | tf_op jit(solution)/shard_map/psum | solution.py:53
  406.4 1.1 fusion.74
  407.8 5.8 %cholesky.224 = f32[64,64]{1,0:T(8,128)S(1)} custom-call(f32[64,64]{1,0:T(8,128)S(1)} %fusion.23), custom_call_target="Cholesky" | custom-call | tf_op jit(solution)/shard_map/jit(cholesky)/cholesky | solution.py:21
  415.0 4.9 custom-call.26
  420.1 1.1 fusion.76
  421.5 5.8 %cholesky.235 = f32[64,64]{1,0:T(8,128)S(1)} custom-call(f32[64,64]{1,0:T(8,128)S(1)} %fusion.19), custom_call_target="Cholesky" | custom-call | tf_op jit(solution)/shard_map/jit(cholesky)/cholesky | solution.py:21
  428.7 4.9 custom-call.27
  433.9 1.9 convolution_bitcast_fusion.2
  435.8 53.8 %all-gather.8.cloned.1.call-done = f32[64,64,256]{1,2,0:T(8,128)} async-done(((f32[64,64,32]{1,2,0:T(8,128)}), f32[64,64,256]{1,2,0:T(8,128)}) %all-gather.8.cloned.1.call-update) | async-done | bytes 4194320 | tf_op jit(solution)/shard_map/all_gather | solution.py:56
  489.6 11.5 %fusion.13 = f32[64,256,32]{1,2,0:T(8,128)S(1)} fusion(f32[64,64,256]{1,2,0:T(8,128)} %all-gather.8.cloned.1.call-done, f32[64,128]{1,0:T(8,128)S(1)} %fusion.16, s32[]{:T(128)S(6)} %select_n.20), kind=kOutput, calls=%fused_computation.25 | convolution fusion | flops 402653184 | bytes 6324228 | tf_op jit(solution)/shard_map/cu,sue->sce/dot_general | solution.py:59
  501.1 1.2 copy.75
  502.3 1.2 fusion.39
  504.2 0.9 copy.67
  505.1 1.0 convolution_bitcast_fusion.1
  506.1 3.8 copy.74
  510.0 11.8 %convolution_subtract_fusion = f32[16,32,16,256]{3,2,1,0:T(8,128)} fusion(f32[16,32,16,256]{3,2,1,0:T(8,128)} %param.16, f32[16,32,16,32]{3,2,1,0:T(8,128)} %bitcast.200, f32[32,256]{1,0:T(8,128)S(1)} %convolution_multiply_fusion), kind=kOutput, calls=%fused_computation.3 | convolution fusion | flops 807403520 | bytes 17858560 | tf_op jit(solution)/shard_map/dot_general | solution.py:63
  (87 shorter events, 19.1 us)
Async XLA Ops:
  6.5 147.4 %copy-start = (f32[256,32]{0,1:T(8,128)S(1)}, f32[256,32]{0,1:T(8,128)}, u32[]{:S(2)}) copy-start(f32[256,32]{0,1:T(8,128)} %param.17) | copy-start | bytes 98308
  6.5 147.4 %all-reduce.4.cloned.1.call-start = ((), (), s32[]{:S(2)}) async-start(), calls=%async_computation | async-start | bytes 524288 | tf_op jit(solution)/shard_map/psum | solution.py:34
  24.3 57.9 %copy-start.4 = (f32[16,8]{0,1:T(8,128)S(1)}, f32[16,8]{0,1:T(8,128)}, u32[]{:S(2)}) copy-start(f32[16,8]{0,1:T(8,128)} %param.18) | copy-start | bytes 1540
  24.3 201.5 %all-gather.4.cloned.1.call-start = ((), (), s32[]{:S(2)}) async-start(), calls=%async_computation.1 | async-start | bytes 4718592 | tf_op jit(solution)/shard_map/all_gather | solution.py:42
  189.9 77.9 %all-reduce.6.cloned.1.call-start = ((), (), s32[]{:S(2)}) async-start(), calls=%async_computation.2 | async-start | bytes 131072 | tf_op jit(solution)/shard_map/psum | solution.py:46
  233.3 113.9 %all-gather.6.cloned.1.call-start = ((), (), s32[]{:S(2)}) async-start(), calls=%async_computation.3 | async-start | bytes 2621440 | tf_op jit(solution)/shard_map/all_gather | solution.py:51
  233.4 34.4 %copy-start.2 = (f32[128,64]{0,1:T(8,128)S(1)}, f32[128,64]{0,1:T(8,128)}, u32[]{:S(2)}) copy-start(f32[128,64]{0,1:T(8,128)} %param.19) | copy-start | bytes 98308
  300.9 105.6 %copy-start.3 = (f32[128,64]{0,1:T(8,128)S(1)}, f32[128,64]{0,1:T(8,128)}, u32[]{:S(2)}) copy-start(f32[128,64]{0,1:T(8,128)} %param.20) | copy-start | bytes 98308
  301.7 104.7 %all-reduce.8.cloned.1.call-start = ((), (), s32[]{:S(2)}) async-start(), calls=%async_computation.4 | async-start | bytes 131072 | tf_op jit(solution)/shard_map/psum | solution.py:53
  354.3 135.3 %all-gather.8.cloned.1.call-start = ((), (), s32[]{:S(2)}) async-start(), calls=%async_computation.5 | async-start | bytes 9437184 | tf_op jit(solution)/shard_map/all_gather | solution.py:56
  510.0 11.8 %copy-start.1 = (f32[256,32]{0,1:T(8,128)S(1)}, f32[256,32]{0,1:T(8,128)}, u32[]{:S(2)}) copy-start(f32[256,32]{0,1:T(8,128)} %param.17) | copy-start | bytes 98308
Sparse Core Ops, SparseCore 0:
  24.4 129.5 all-reduce.3
  190.1 35.6 all-gather.3
  233.5 34.2 all-reduce.5
  301.9 45.3 all-gather.5
  354.4 51.9 all-reduce.7
  435.9 53.6 all-gather.7
where the time goes:
time: 537 us; the launch traced here: 529 us
  waiting for transfers between devices  278 us (52%)
  matrix products  100 us (19%)
  other arithmetic  67.3 us (13%)
  blocking collectives  42.4 us (8%)
  local copies, waits for them, and re-layouts  25.1 us (5%)
  between operations  15.5 us (3%)
    psum x1, waiting for transfers between devices, local(): lax.psum((local_frames, local_sends), ('row', 'col'))  65.3 us
    all_gather x1, waiting for transfers between devices, local(): third = lax.all_gather(third_slice, 'row', axis=2, tiled=True)  53.8 us
    psum x1, waiting for transfers between devices, local(): gram_cols = lax.psum(local_cols, 'row')  49.1 us
    all_gather x1, waiting for transfers between devices, local(): across = lax.all_gather(own_slice, 'col', axis=1, tiled=True)  45 us
    psum x1, blocking collectives, local(): lax.psum((local_frames, local_sends), ('row', 'col'))  42.4 us
    another operation x24, other arithmetic, orthonormal(): factor = jnp.linalg.cholesky(inner)  36.3 us
    all_gather x1, waiting for transfers between devices, local(): gathered = lax.all_gather(core, 'row', axis=0, tiled=True)  35.5 us
    another operation x16, other arithmetic, orthonormal(): basis = jax.scipy.linalg.solve_triangular(factor, image.T, lower=True).T  31 us
  transfers between devices with their start and end apart: 6, of which 6 were waited for; matrix products, arithmetic and copies ran while one was open for 6% of the time, Pallas kernels for 0%

commit v1 on v0

--- a/solution.py
+++ b/solution.py
@@ -10,6 +10,11 @@
 RS = 64
 ITERS = 2
 CORE_W = 256
+
+
+def summed_here(x, mesh_axis):
+    parts = lax.all_gather(x, mesh_axis)
+    return jnp.sum(parts, axis=0)
 
 
 def orthonormal(gram, start):
@@ -43,7 +48,7 @@
     total_rows = gathered.shape[0]
     unfolded = gathered.reshape(total_rows, -1)
     local_rows = jnp.dot(unfolded, unfolded.T, precision=high)
-    gram_rows = lax.psum(local_rows, "col")
+    gram_rows = summed_here(local_rows, "col")
     basis_rows = orthonormal(gram_rows, start_rows)
     second = jnp.dot(basis_rows.T, unfolded, precision=high).reshape(RS, cols_dev, CORE_W)
     width = CORE_W // lax.axis_size("row")

time: 537 us -> 520 us (0.968)
  waiting for transfers between devices: 278 us -> 250 us
  blocking collectives: 42.4 us -> 56.3 us
    psum x1 -> x0, waiting for transfers between devices: 28.8 us -> none  [local(): gram_rows = lax.psum(local_rows, 'col')]
    all_gather x0 -> x1, blocking collectives: none -> 13.9 us  [summed_here(): parts = lax.all_gather(x, mesh_axis)]
  transfers between devices with their start and end apart: 6 -> 5, of which waited for: 6 -> 5; matrix products, arithmetic and copies ran while one was open for 6% -> 5% of each run, Pallas kernels for 0% -> 0%
where the time goes in v1:
time: 520 us; the launch traced here: 512 us
  waiting for transfers between devices  250 us (48%)
  matrix products  97.8 us (19%)
  other arithmetic  67.1 us (13%)
  blocking collectives  56.3 us (11%)
  local copies, waits for them, and re-layouts  25.1 us (5%)
  between operations  15.1 us (3%)
    psum x1, waiting for transfers between devices, local(): lax.psum((local_frames, local_sends), ('row', 'col'))  65.3 us
    all_gather x1, waiting for transfers between devices, local(): third = lax.all_gather(third_slice, 'row', axis=2, tiled=True)  53.8 us
    psum x1, waiting for transfers between devices, local(): gram_cols = lax.psum(local_cols, 'row')  49.1 us
    all_gather x1, waiting for transfers between devices, local(): across = lax.all_gather(own_slice, 'col', axis=1, tiled=True)  45.9 us
    psum x1, blocking collectives, local(): lax.psum((local_frames, local_sends), ('row', 'col'))  42.4 us
    another operation x24, other arithmetic, orthonormal(): factor = jnp.linalg.cholesky(inner)  36.1 us
    all_gather x1, waiting for transfers between devices, local(): gathered = lax.all_gather(core, 'row', axis=0, tiled=True)  35.5 us
    another operation x16, other arithmetic, orthonormal(): basis = jax.scipy.linalg.solve_triangular(factor, image.T, lower=True).T  30.9 us
  transfers between devices with their start and end apart: 5, of which 5 were waited for; matrix products, arithmetic and copies ran while one was open for 5% of the time, Pallas kernels for 0%

profile of v1, /device:TPU:0, one launch (start us, length us, event | category | flops | bytes accessed | tf_op | source)
XLA Modules:
  0.0 511.9 jit_solution(5196639394590275542)
XLA Ops:
  6.5 17.7 %convolution_bitcast_fusion.4 = f32[256,256]{1,0:T(8,128)} fusion(f32[16,32,16,256]{3,2,1,0:T(8,128)} %param.16), kind=kOutput, calls=%fused_computation.9 | convolution fusion | flops 6442450944 | bytes 8650752 | tf_op jit(solution)/shard_map/pt,pu->tu/dot_general | solution.py:37
  24.3 14.1 %convolution_bitcast_fusion.6 = f32[16,16]{1,0:T(8,128)S(1)} fusion(f32[16,32,16,256]{3,2,1,0:T(8,128)} %param.16), kind=kOutput, calls=%fused_computation.13 | convolution fusion | flops 402653184 | bytes 8389632 | tf_op jit(solution)/shard_map/pkt,pjt->kj/dot_general | solution.py:38
  39.8 42.4 %psum.21 = f32[16,16]{1,0:T(8,128)S(1)} all-reduce(f32[16,16]{1,0:T(8,128)S(1)} %convolution_bitcast_fusion.6), channel_id=1, replica_groups=mesh['row'=8,'col'=4] {'row','col'}, use_global_device_ids=true, to_apply=%region_0.0 | all-reduce | flops 256 | bytes 2048 | tf_op jit(solution)/shard_map/psum | solution.py:39
  82.5 0.7 cholesky.158
  83.2 0.7 compare_reduce_fusion.7
  85.7 0.7 cholesky.169
  88.6 65.3 %all-reduce.3.cloned.1.call-done = f32[256,256]{1,0:T(8,128)} async-done(((f32[256,256]{1,0:T(8,128)}), f32[256,256]{1,0:T(8,128)}) %all-reduce.3.cloned.1.call-update) | async-done | bytes 262160 | tf_op jit(solution)/shard_map/psum | solution.py:39
  153.9 1.3 fusion.66
  155.5 2.9 cholesky.180
  159.7 2.4 custom-call.22
  162.4 1.3 fusion.68
  164.0 2.9 cholesky.191
  168.2 2.4 custom-call.23
  170.9 9.9 %convolution_bitcast_fusion = f32[8192,32]{0,1:T(8,128)S(1)} fusion(f32[32,256]{1,0:T(8,128)S(1)} %convolution_multiply_fusion, f32[8192,256]{1,0:T(8,128)} %bitcast.200), kind=kOutput, calls=%fused_computation | convolution fusion | flops 805306368 | bytes 9469952 | tf_op jit(solution)/shard_map/dot_general | solution.py:44
  180.8 2.7 copy.54
  183.5 3.2 copy.55
  187.4 0.8 copy.56
  188.8 1.1 copy.57
  190.2 35.5 %all-gather.5.cloned.1.call-done = f32[128,32,256]{2,0,1:T(8,128)} async-done(((f32[16,32,256]{2,0,1:T(8,128)}), f32[128,32,256]{2,0,1:T(8,128)}) %all-gather.5.cloned.1.call-update) | async-done | bytes 4194320 | tf_op jit(solution)/shard_map/all_gather | solution.py:47
  225.7 6.9 %convolution_bitcast_fusion.5 = f32[128,128]{1,0:T(8,128)S(1)} fusion(f32[128,32,256]{2,0,1:T(8,128)} %all-gather.5.cloned.1.call-done), kind=kOutput, calls=%fused_computation.11 | convolution fusion | flops 1610612736 | bytes 4259840 | tf_op jit(solution)/shard_map/dot_general | solution.py:50
  232.7 13.9 %all-gather = f32[512,128]{1,0:T(8,128)S(1)} all-gather(f32[128,128]{1,0:T(8,128)S(1)} %convolution_bitcast_fusion.5), channel_id=2, replica_groups=mesh['row'=8,'col'=4] {'col'}, dimensions={0}, use_global_device_ids=true | all-gather | bytes 327680 | tf_op jit(solution)/shard_map/all_gather | solution.py:16
  247.2 5.8 %cholesky.202 = f32[64,64]{1,0:T(8,128)S(1)} custom-call(f32[64,64]{1,0:T(8,128)S(1)} %fusion.32), custom_call_target="Cholesky" | custom-call | tf_op jit(solution)/shard_map/jit(cholesky)/cholesky | solution.py:26
  254.4 4.9 custom-call.24
  260.1 5.8 %cholesky.213 = f32[64,64]{1,0:T(8,128)S(1)} custom-call(f32[64,64]{1,0:T(8,128)S(1)} %fusion.28), custom_call_target="Cholesky" | custom-call | tf_op jit(solution)/shard_map/jit(cholesky)/cholesky | solution.py:26
  267.3 4.9 custom-call.25
  272.4 5.6 %copy.60 = f32[128,32,256]{0,2,1:T(8,128)} copy(f32[128,32,256]{2,0,1:T(8,128)} %all-gather.5.cloned.1.call-done) | data formatting | bytes 8388608 | tf_op jit(solution)/shard_map/all_gather | solution.py:47
  278.0 5.4 %fusion = f32[64,32,256]{0,2,1:T(8,128)S(1)} fusion(f32[128,32,256]{0,2,1:T(8,128)} %copy.60, f32[64,128]{1,0:T(8,128)S(1)} %fusion.25), kind=kOutput, calls=%fused_computation.1 | convolution fusion | flops 805306368 | bytes 6324224 | tf_op jit(solution)/shard_map/dot_general | solution.py:53
  283.4 0.8 constant_dynamic-slice_fusion
  284.7 45.9 %all-gather.7.cloned.1.call-done = f32[64,128,32]{0,2,1:T(8,128)} async-done(((f32[64,32,32]{0,2,1:T(8,128)}), f32[64,128,32]{0,2,1:T(8,128)}) %all-gather.7.cloned.1.call-update) | async-done | bytes 1048592 | tf_op jit(solution)/shard_map/all_gather | solution.py:56
  330.6 7.0 %fusion.4 = f32[128,128]{1,0:T(8,128)} fusion(f32[64,128,32]{0,2,1:T(8,128)} %all-gather.7.cloned.1.call-done), kind=kOutput, calls=%fused_computation.10 | convolution fusion | flops 402653184 | bytes 1114112 | tf_op jit(solution)/shard_map/sce,sde->cd/dot_general | solution.py:57
  337.7 3.0 copy.65
  340.7 49.1 %all-reduce.5.cloned.1.call-done = f32[128,128]{1,0:T(8,128)} async-done(((f32[128,128]{1,0:T(8,128)}), f32[128,128]{1,0:T(8,128)}) %all-reduce.5.cloned.1.call-update) | async-done | bytes 65552 | tf_op jit(solution)/shard_map/psum | solution.py:58
  389.8 1.1 fusion.74
  391.1 5.8 %cholesky.224 = f32[64,64]{1,0:T(8,128)S(1)} custom-call(f32[64,64]{1,0:T(8,128)S(1)} %fusion.23), custom_call_target="Cholesky" | custom-call | tf_op jit(solution)/shard_map/jit(cholesky)/cholesky | solution.py:26
  398.3 4.9 custom-call.26
  403.5 1.1 fusion.76
  404.9 5.8 %cholesky.235 = f32[64,64]{1,0:T(8,128)S(1)} custom-call(f32[64,64]{1,0:T(8,128)S(1)} %fusion.19), custom_call_target="Cholesky" | custom-call | tf_op jit(solution)/shard_map/jit(cholesky)/cholesky | solution.py:26
  412.0 4.9 custom-call.27
  417.2 1.9 convolution_bitcast_fusion.2
  419.2 53.8 %all-gather.9.cloned.1.call-done = f32[64,64,256]{1,2,0:T(8,128)} async-done(((f32[64,64,32]{1,2,0:T(8,128)}), f32[64,64,256]{1,2,0:T(8,128)}) %all-gather.9.cloned.1.call-update) | async-done | bytes 4194320 | tf_op jit(solution)/shard_map/all_gather | solution.py:61
  473.0 11.5 %fusion.13 = f32[64,256,32]{1,2,0:T(8,128)S(1)} fusion(f32[64,64,256]{1,2,0:T(8,128)} %all-gather.9.cloned.1.call-done, f32[64,128]{1,0:T(8,128)S(1)} %fusion.16, s32[]{:T(128)S(6)} %select_n.20), kind=kOutput, calls=%fused_computation.25 | convolution fusion | flops 402653184 | bytes 6324228 | tf_op jit(solution)/shard_map/cu,sue->sce/dot_general | solution.py:64
  484.5 1.2 copy.75
  485.7 1.2 fusion.39
  486.8 0.7 reshape.64
  487.5 0.9 copy.67
  488.4 1.0 convolution_bitcast_fusion.1
  489.5 3.8 copy.74
  493.3 11.8 %convolution_subtract_fusion = f32[16,32,16,256]{3,2,1,0:T(8,128)} fusion(f32[16,32,16,256]{3,2,1,0:T(8,128)} %param.16, f32[16,32,16,32]{3,2,1,0:T(8,128)} %bitcast.201, f32[32,256]{1,0:T(8,128)S(1)} %convolution_multiply_fusion), kind=kOutput, calls=%fused_computation.3 | convolution fusion | flops 807403520 | bytes 17858560 | tf_op jit(solution)/shard_map/dot_general | solution.py:68
  (86 shorter events, 18.0 us)
Async XLA Ops:
  6.5 147.4 %copy-start = (f32[256,32]{0,1:T(8,128)S(1)}, f32[256,32]{0,1:T(8,128)}, u32[]{:S(2)}) copy-start(f32[256,32]{0,1:T(8,128)} %param.17) | copy-start | bytes 98308
  6.5 147.4 %all-reduce.3.cloned.1.call-start = ((), (), s32[]{:S(2)}) async-start(), calls=%async_computation | async-start | bytes 524288 | tf_op jit(solution)/shard_map/psum | solution.py:39
  24.3 57.9 %copy-start.4 = (f32[16,8]{0,1:T(8,128)S(1)}, f32[16,8]{0,1:T(8,128)}, u32[]{:S(2)}) copy-start(f32[16,8]{0,1:T(8,128)} %param.18) | copy-start | bytes 1540
  24.3 201.5 %all-gather.5.cloned.1.call-start = ((), (), s32[]{:S(2)}) async-start(), calls=%async_computation.1 | async-start | bytes 4718592 | tf_op jit(solution)/shard_map/all_gather | solution.py:47
  189.9 140.6 %all-gather.7.cloned.1.call-start = ((), (), s32[]{:S(2)}) async-start(), calls=%async_computation.2 | async-start | bytes 2621440 | tf_op jit(solution)/shard_map/all_gather | solution.py:56
  190.2 56.4 %copy-start.2 = (f32[128,64]{0,1:T(8,128)S(1)}, f32[128,64]{0,1:T(8,128)}, u32[]{:S(2)}) copy-start(f32[128,64]{0,1:T(8,128)} %param.19) | copy-start | bytes 98308
  283.4 106.4 %copy-start.3 = (f32[128,64]{0,1:T(8,128)S(1)}, f32[128,64]{0,1:T(8,128)}, u32[]{:S(2)}) copy-start(f32[128,64]{0,1:T(8,128)} %param.20) | copy-start | bytes 98308
  284.2 105.5 %all-reduce.5.cloned.1.call-start = ((), (), s32[]{:S(2)}) async-start(), calls=%async_computation.3 | async-start | bytes 131072 | tf_op jit(solution)/shard_map/psum | solution.py:58
  337.6 135.3 %all-gather.9.cloned.1.call-start = ((), (), s32[]{:S(2)}) async-start(), calls=%async_computation.4 | async-start | bytes 9437184 | tf_op jit(solution)/shard_map/all_gather | solution.py:61
  493.3 11.8 %copy-start.1 = (f32[256,32]{0,1:T(8,128)S(1)}, f32[256,32]{0,1:T(8,128)}, u32[]{:S(2)}) copy-start(f32[256,32]{0,1:T(8,128)} %param.17) | copy-start | bytes 98308
Sparse Core Ops, SparseCore 0:
  24.4 129.5 all-reduce.2
  190.1 35.6 all-gather.4
  284.4 46.1 all-gather.6
  337.8 51.9 all-reduce.4
  419.3 53.6 all-gather.8
